TPU v7x, 128 devices: a whole 4x4x4 slice. The times are simulated.
128 devices in a mesh: row: 8 (over y, x_hi), col: 16 (over z, x_lo, core).
Axes of the slice: x: 4 (x_hi: 2, x_lo: 2; x = x_hi * 2 + x_lo), y: 4, z: 4, core: 2. Of those that a mesh axis runs over, the one named last changes fastest.
Arguments:
- h_slab: bfloat16 [4096, 96000], P('row', 'col'), may hold values from -0.01953125 to 0.01953125
- vectors: bfloat16 [96000, 1024], P('col'), may hold values from -6 to 6
- left_rows: bfloat16 [4096, 1024], P('row'), may hold values from -0.09375 to 0.09375
Outputs:
- projected: float32 [1024, 1024], replicated
All inputs are finite; a program needn't handle non-finite values.
Results may differ from a plain program's by a relative error of at most 0.0003.
Values sent between devices are 32-bit elements; how exact they have to be, the bound alone decides.
A program may use at most 128 MiB of HBM per device.

v0:
```python
import jax
import jax.numpy as jnp
from jax import lax
from jax.sharding import PartitionSpec as P


def cut_along(shard, dim, devices):
    before, after = (shard.shape[:dim], shard.shape[dim + 1 :])
    return jnp.moveaxis(shard.reshape(*before, devices, -1, *after), dim, 0)


def sum_at_owner(shard, axis, dim):
    devices = lax.axis_size(axis)
    parts = lax.all_to_all(cut_along(shard, dim, devices), axis, 0, 0, tiled=True)
    return jnp.sum(parts, axis=0)


def copy_for_each(shard, axis):
    copies = jnp.broadcast_to(shard, (lax.axis_size(axis), *shard.shape))
    return lax.all_to_all(copies, axis, split_axis=0, concat_axis=0, tiled=True)


def over_copies(shard, axis):
    everything = copy_for_each(shard, axis)
    return jnp.sum(everything, axis=0)


def body(h_slab, vectors, left_rows):
    left_wide = left_rows.astype(jnp.float32)
    shared = sum_at_owner(
        lax.dot_general(
            vectors, h_slab, (((0,), (1,)), ((), ())), preferred_element_type=jnp.float32
        ),
        "col",
        0,
    )
    local_part = lax.dot_general(
        left_wide,
        shared,
        (((0,), (1,)), ((), ())),
        precision=lax.Precision.HIGHEST,
        preferred_element_type=jnp.float32,
    )
    summed = over_copies(local_part, "row")
    projected = lax.all_gather(summed, "col", axis=1, tiled=True)
    return projected


def solution(mesh):
    in_specs = (P("row", "col"), P("col", None), P("row", None))
    out_specs = P()
    return jax.shard_map(body, mesh=mesh, in_specs=in_specs, out_specs=out_specs, check_vma=False)
```

profile of v0, /device:TPU:1, one launch (start us, length us, event | category | flops | bytes accessed | tf_op | source)
XLA Modules:
  0.0 134.7 jit_solution(6688112927159903373)
XLA Ops:
  6.5 0.0 copy-start
  6.5 0.0 all-gather.2.cloned.1.call-start
  6.5 11.5 %fusion = f32[1024,512]{1,0:T(8,128)S(1)} fusion(bf16[6000,1024]{1,0:T(8,128)(2,1)} %param.4, bf16[512,6000]{0,1:T(8,128)(2,1)} %param.3), kind=kOutput, calls=%fused_computation.1 | convolution fusion | flops 6291456000 | bytes 20529152 | tf_op jit(solution)/shard_map/dot_general | solution.py:31
  18.0 34.0 %all_to_all.10 = f32[16,64,512]{2,1,0:T(8,128)S(1)} all-to-all(f32[16,64,512]{2,1,0:T(8,128)S(1)} %bitcast.7), channel_id=1, replica_groups=mesh['row'=8,'col'=16] {'col'}, dimensions={0} | all-to-all | bytes 4194304 | tf_op jit(solution)/shard_map/all_to_all | solution.py:14
  52.1 0.2 reduce_sum.18
  52.2 0.0 copy-done
  52.3 0.7 convolution_bitcast_fusion
  52.9 0.2 broadcast_in_dim.3
  53.2 33.1 %all_to_all.11 = f32[8,1024,64]{1,2,0:T(8,128)S(1)} all-to-all(f32[8,1024,64]{1,2,0:T(8,128)S(1)} %broadcast_in_dim.3), channel_id=1, replica_groups=mesh['row'=8,'col'=16] {'row'}, dimensions={0} | all-to-all | bytes 4194304 | tf_op jit(solution)/shard_map/all_to_all | solution.py:20
  86.3 0.8 reduce_sum.19
  87.2 0.0 all-gather.2.cloned.1.call-update
  87.2 35.4 %all-gather.2.cloned.1.call-done = f32[1024,1024]{0,1:T(8,128)} async-done(((f32[1024,64]{0,1:T(8,128)}), f32[1024,1024]{0,1:T(8,128)}) %all-gather.2.cloned.1.call-update) | async-done | bytes 4194320 | tf_op jit(solution)/shard_map/all_gather | solution.py:45
  122.6 5.3 %copy.5 = f32[1024,1024]{1,0:T(8,128)} copy(f32[1024,1024]{0,1:T(8,128)} %all-gather.2.cloned.1.call-done) | data formatting | bytes 8388608 | tf_op jit(solution)/shard_map/all_gather | solution.py:45
Async XLA Ops:
  6.5 45.7 %copy-start = (bf16[512,1024]{1,0:T(8,128)(2,1)S(1)}, bf16[512,1024]{1,0:T(8,128)(2,1)}, u32[]{:S(2)}) copy-start(bf16[512,1024]{1,0:T(8,128)(2,1)} %param.5) | copy-start | bytes 3145732
  6.5 116.0 %all-gather.2.cloned.1.call-start = ((), (), s32[]{:S(2)}) async-start(), calls=%async_computation.2 | async-start | bytes 4456448 | tf_op jit(solution)/shard_map/all_gather | solution.py:45
Sparse Core Ops, SparseCore 0:
  87.3 35.1 all-gather.1
where the time goes:
time: 135 us
  blocking collectives  67.2 us (50%)
  waiting for transfers between devices  35.4 us (26%)
  between operations  13.4 us (10%)
  matrix products  12.1 us (9%)
  local copies, waits for them, and re-layouts  5.58 us (4%)
    all_gather x1, waiting for transfers between devices, body(): projected = lax.all_gather(summed, 'col', axis=1, tiled=True)  35.4 us
    all_to_all x1, blocking collectives, sum_at_owner(): lax.all_to_all(cut_along(shard, dim, devices), axis, 0, 0, tiled=True)  34 us
    all_to_all x1, blocking collectives, copy_for_each(): return lax.all_to_all(copies, axis, split_axis=0, concat_axis=0, tiled=True)  33.1 us
    dot_general x1, matrix products, body(): lax.dot_general(vectors, h_slab, (((0,), (1,)), ((), ())), preferred_elem...  11.5 us
    all_gather x1, local copies, waits for them, and re-layouts, body(): projected = lax.all_gather(summed, 'col', axis=1, tiled=True)  5.34 us
  transfers between devices with their start and end apart: 1, of which 1 were waited for; matrix products, arithmetic and copies ran while one was open for 0% of the time, Pallas kernels for 0%

commit v1 on v0

v1 whole, which is shorter than its diff:
```python
import functools

import jax
import jax.numpy as jnp
from jax import lax
from jax.experimental import pallas as pl
from jax.experimental.pallas import tpu as pltpu
from jax.sharding import PartitionSpec as P

MESH = pl.DeviceIdType.MESH
F32 = jnp.float32
BF16 = jnp.bfloat16
DEPTH = 6000
ROWS = 512
HALF = 256
NVEC = 1024
CUTS = ((0, 2048), (2048, 4096), (4096, 6000))
A, A2 = 144, 72
B, B2 = 112, 56
ROTATIONS = ((0, 24), (24, 24), (48, 16))
NMSG = 160
CONTRACT0 = (((0,), (0,)), ((), ()))


def kernel(h_hbm, v_hbm, l_hbm, out, h, v, l, p, dr, zr1, zr2, xb, zb1, zb2, xa, pf, pfr, bhl, rp, rr, lsem, ssem, rsem):
    row, col = lax.axis_index("row"), lax.axis_index("col")
    y, xh = row // 2, row % 2
    z, xl, c = col // 4, (col // 2) % 2, col % 2
    x = xh * 2 + xl

    def dev(dx=0, dy=0, dz=0, core=None, px=None):
        nx = (x + dx) % 4 if px is None else px
        ny, nz = (y + dy) % 4, (z + dz) % 4
        nc = c if core is None else core
        return (ny * 2 + nx // 2, nz * 4 + (nx % 2) * 2 + nc)

    partner = dev(core=1 - c)
    mate = dev(px=xh * 2 + 1 - xl)

    zs = [(z + 2) % 4, (z + 1) % 4, (z + 3) % 4, z]
    lanes = [pl.ds(pl.multiple_of(q * 256, 256), 256) for q in zs]
    loads = []

    def load(src, dst):
        cp = pltpu.make_async_copy(src, dst, lsem.at[len(loads)])
        cp.start()
        loads.append(cp)
        return cp

    first = []
    for lo, hi in CUTS:
        k = pl.ds(lo, hi - lo)
        first.append((load(h_hbm.at[k, :], h.at[k, :]), load(v_hbm.at[k, lanes[0]], v.at[0, k, :])))
    rest = [load(v_hbm.at[:, lanes[s]], v.at[s]) for s in (1, 2, 3)]
    lload = load(l_hbm.at[:, pl.ds(pl.multiple_of(c * 512, 512), 512)], l)

    barrier = pltpu.get_barrier_semaphore()
    peers = [partner]
    for d in (1, 2, 3):
        peers += [dev(dx=d), dev(dy=d), dev(dz=d), dev(dx=2, dy=d)]
    for peer in peers:
        pl.semaphore_signal(barrier, inc=1, device_id=peer, device_id_type=MESH)

    sent = []

    def send(src, dst, device):
        i = len(sent)
        rc = pltpu.make_async_remote_copy(
            src_ref=src, dst_ref=dst, send_sem=ssem.at[i], recv_sem=rsem.at[i], device_id=device, device_id_type=MESH
        )
        rc.start()
        sent.append(rc)
        return rc

    def dot(s, lo, hi):
        k = pl.ds(lo, hi - lo)
        return lax.dot_general(h[k, :], v[s, k, :], CONTRACT0, preferred_element_type=F32).reshape(2, HALF, 256)

    def swap(s):
        return send(p.at[s, 1 - c], dr.at[s], partner)

    def settle(s, rc):
        rc.wait_recv()
        p[s, c] = p[s, c] + dr[s]

    ours = pl.ds(pl.multiple_of(xl * 128, 128), 128)
    theirs = pl.ds(pl.multiple_of(128 - xl * 128, 128), 128)

    def xb_send(s):
        return send(p.at[s, c, pl.ds(A, B), theirs], xb.at[s], mate)

    def xb_settle(s, rc):
        rc.wait_recv()
        p[s, c, pl.ds(A, B), ours] = p[s, c, pl.ds(A, B), ours] + xb[s]

    up, down = dev(dz=1), dev(dz=3)
    a_lo, a_hi = pl.ds(0, A2), pl.ds(A2, A2)
    b_lo, b_hi = pl.ds(A, B2), pl.ds(A + B2, B2)

    for i, (lo, hi) in enumerate(CUTS):
        first[i][0].wait()
        first[i][1].wait()
        if i == 0:
            p[0] = dot(0, lo, hi)
        else:
            p[0] = p[0] + dot(0, lo, hi)
    pl.semaphore_wait(barrier, len(peers))
    d0 = swap(0)
    rest[0].wait()
    p[1] = dot(1, 0, DEPTH)
    d1 = swap(1)
    settle(0, d0)
    za1u = send(p.at[0, c, a_lo, :], zr1.at[0], up)
    za1d = send(p.at[0, c, a_hi, :], zr1.at[1], down)
    xb0 = xb_send(0)
    rest[1].wait()
    p[2] = dot(2, 0, DEPTH)
    d2 = swap(2)
    settle(1, d1)
    za2u = send(p.at[1, c, a_hi, :], zr2.at[0, 1], up)
    xb1 = xb_send(1)
    rest[2].wait()
    p[3] = dot(3, 0, DEPTH)
    d3 = swap(3)
    settle(2, d2)
    za2d = send(p.at[2, c, a_lo, :], zr2.at[1, 0], down)
    xb2 = xb_send(2)
    xb_settle(0, xb0)
    zb1u = send(p.at[0, c, b_lo, ours], zb1.at[0], up)
    zb1d = send(p.at[0, c, b_hi, ours], zb1.at[1], down)
    za1u.wait_recv()
    p[1, c, a_lo, :] = p[1, c, a_lo, :] + zr1[0]
    za3u = send(p.at[1, c, a_lo, :], zr2.at[0, 0], up)
    za1d.wait_recv()
    p[2, c, a_hi, :] = p[2, c, a_hi, :] + zr1[1]
    za3d = send(p.at[2, c, a_hi, :], zr2.at[1, 1], down)
    settle(3, d3)
    xb3 = xb_send(3)
    xb_settle(1, xb1)
    zb2u = send(p.at[1, c, b_hi, ours], zb2.at[0, 1], up)
    xb_settle(2, xb2)
    zb2d = send(p.at[2, c, b_lo, ours], zb2.at[1, 0], down)
    zb1u.wait_recv()
    p[1, c, b_lo, ours] = p[1, c, b_lo, ours] + zb1[0]
    zb3u = send(p.at[1, c, b_lo, ours], zb2.at[0, 0], up)
    zb1d.wait_recv()
    p[2, c, b_hi, ours] = p[2, c, b_hi, ours] + zb1[1]
    zb3d = send(p.at[2, c, b_hi, ours], zb2.at[1, 1], down)
    for rc in (za2u, za3u, za2d, za3d):
        rc.wait_recv()
    p[3, c, pl.ds(0, A), :] = p[3, c, pl.ds(0, A), :] + zr2[0].reshape(A, 256) + zr2[1].reshape(A, 256)
    xas = send(p.at[3, c, pl.ds(0, A), theirs], xa, mate)
    xb_settle(3, xb3)
    for rc in (zb2u, zb3u, zb2d, zb3d):
        rc.wait_recv()
    pf[pl.ds(A, B), :] = p[3, c, pl.ds(A, B), ours] + zb2[0].reshape(B, 128) + zb2[1].reshape(B, 128)
    fb = send(pf.at[pl.ds(A, B), :], pfr.at[pl.ds(A, B), :], partner)
    xas.wait_recv()
    pf[pl.ds(0, A), :] = p[3, c, pl.ds(0, A), ours] + xa[...]
    fa = send(pf.at[pl.ds(0, A), :], pfr.at[pl.ds(0, A), :], partner)

    def split(value, half):
        hi = value.astype(BF16)
        bhl[half, :, pl.ds(0, 128)] = hi
        bhl[half, :, pl.ds(128, 128)] = (value - hi.astype(F32)).astype(BF16)

    split(pf[...], c)
    lload.wait()
    fb.wait_recv()
    fa.wait_recv()
    split(pfr[...], 1 - c)
    both = lax.dot_general(l[...], bhl[...].reshape(ROWS, 256), CONTRACT0, preferred_element_type=F32)
    rp[...] = (both[:, :128] + both[:, 128:]).reshape(8, 64, 128)

    adds = []
    for dx in (0, 2):
        for dy in (0, 1, 3, 2):
            if dx or dy:
                their_row = ((y + dy) % 4) * 2 + (xh + dx // 2) % 2
                adds.append(send(rp.at[their_row], rr.at[len(adds)], dev(dx=dx, dy=dy)))
    total = rp[row]
    for i, rc in enumerate(adds):
        rc.wait_recv()
        total = total + rr[i]

    def lane(qz, qx):
        return pl.ds(pl.multiple_of(qz * 256 + (qx % 2) * 128, 128), 128)

    def wide(qz):
        return pl.ds(pl.multiple_of(qz * 256, 256), 256)

    out[c, y, xh, :, lane(z, x)] = total

    R = [pl.ds(a, n) for a, n in ROTATIONS]

    def set_x(d, g, half=None):
        qx = (x + d) % 4
        ys = pl.ds(0, 4) if half is None else pl.ds(2 * half, 2)
        return out.at[c, ys, qx // 2, R[0], lane((z + g) % 4, qx)]

    def set_y(d, g, half=None):
        hs = pl.ds(0, 2) if half is None else pl.ds(half, 1)
        return out.at[c, (y + d) % 4, hs, R[1], wide((z + g) % 4)]

    def set_z(d, g, half=None):
        hs = pl.ds(0, 2) if half is None else pl.ds(half, 1)
        return out.at[c, (y + g) % 4, hs, R[2], wide((z + d) % 4)]

    sets = (set_x, set_y, set_z)
    along = ("dx", "dy", "dz")
    second = ("dz", "dz", "dy")
    block = lambda rows: out.at[c, y, xh, rows, lane(z, x)]
    same = lambda ref, device: send(ref, ref, device)

    low, high = R[0], pl.ds(24, 40)
    s1 = [[], []]
    for d in (1, 3, 2):
        s1[0].append(same(block(low), dev(dy=d)))
        s1[1].append(same(block(high), dev(dx=d)))
    s2 = [{}, {}, {}]
    s3 = [{}, {}, {}]
    fw = [{}, {}, {}]
    last = []

    def onward(t, g):
        ref = sets[t](0, g)
        s3[t][g, 1] = same(ref, dev(**{along[t]: 1}))
        s3[t][g, 3] = same(ref, dev(**{along[t]: 3}))
        last.append(same(ref, partner))

    for t in range(3):
        if t < 2:
            for rc in s1[t]:
                rc.wait_recv()
        for d in (1, 3, 2):
            s2[t][d] = same(sets[t](0, 0), dev(**{second[t]: d}))
        onward(t, 0)
    for d in (1, 3, 2):
        for t in range(3):
            s2[t][d].wait_recv()
            onward(t, (4 - d) % 4)
    for g in (0, 3, 1, 2):
        for t in range(3):
            s3[t][g, 1].wait_recv()
            fw[t][g, 0] = same(sets[t](3, g, 0), dev(**{along[t]: 1}))
            last.append(same(sets[t](3, g), partner))
            s3[t][g, 3].wait_recv()
            fw[t][g, 1] = same(sets[t](1, g, 1), dev(**{along[t]: 3}))
            last.append(same(sets[t](1, g), partner))
    for g in (0, 3, 1, 2):
        for t in range(3):
            fw[t][g, 0].wait_recv()
            fw[t][g, 1].wait_recv()
            last.append(same(sets[t](2, g), partner))
    for rc in last:
        rc.wait_recv()
    for rc in sent:
        rc.wait_send()


def call(h, v, l):
    dma = pltpu.SemaphoreType.DMA
    vmem = pltpu.VMEM
    return pl.pallas_call(
        kernel,
        out_shape=jax.ShapeDtypeStruct((2, 4, 2, 64, NVEC), F32),
        in_specs=[pl.BlockSpec(memory_space=pl.ANY)] * 3,
        out_specs=pl.BlockSpec(memory_space=pltpu.VMEM),
        scratch_shapes=[
            vmem((DEPTH, ROWS), BF16),
            vmem((4, DEPTH, 256), BF16),
            vmem((ROWS, 512), BF16),
            vmem((4, 2, HALF, 256), F32),
            vmem((4, HALF, 256), F32),
            vmem((2, A2, 256), F32),
            vmem((2, 2, A2, 256), F32),
            vmem((4, B, 128), F32),
            vmem((2, B2, 128), F32),
            vmem((2, 2, B2, 128), F32),
            vmem((A, 128), F32),
            vmem((HALF, 128), F32),
            vmem((HALF, 128), F32),
            vmem((2, HALF, 256), BF16),
            vmem((8, 64, 128), F32),
            vmem((7, 64, 128), F32),
            dma((16,)),
            dma((NMSG,)),
            dma((NMSG,)),
        ],
        compiler_params=pltpu.CompilerParams(
            collective_id=0, has_side_effects=True, vmem_limit_bytes=56 * 1024 * 1024
        ),
        cost_estimate=pl.CostEstimate(flops=2 * ROWS * DEPTH * NVEC, bytes_accessed=23000000, transcendentals=0),
    )(h, v, l)


def body(h_slab, vectors, left_rows):
    return call(h_slab.T, vectors, left_rows).reshape(NVEC, NVEC)


def solution(mesh):
    in_specs = (P("row", "col"), P("col", None), P("row", None))
    return jax.shard_map(body, mesh=mesh, in_specs=in_specs, out_specs=P(), check_vma=False)
```

time: 135 us -> 67.7 us (0.50)
  blocking collectives: 67.2 us -> 0 us
  Pallas kernels: 0 us -> 62.8 us
  waiting for transfers between devices: 35.4 us -> 0 us
  between operations: 13.4 us -> 0.01 us
  matrix products: 12.1 us -> 0 us
    all_to_all x2 -> x0, blocking collectives: 67.2 us -> none  [the longest x1 34 us: sum_at_owner(): lax.all_to_all(cut_along(shard, dim, devices), axis, 0, 0, tiled=True)]
    pallas_call x0 -> x1, Pallas kernels: none -> 62.8 us  [call(): pl.pallas_call(kernel, out_shape=jax.ShapeDtypeStruct((2, 4, 2, 64, NVEC)...]
    all_gather x1 -> x0, waiting for transfers between devices: 35.4 us -> none  [body(): projected = lax.all_gather(summed, 'col', axis=1, tiled=True)]
    dot_general x2 -> x0, matrix products: 12.1 us -> none  [the longest x1 11.5 us: body(): lax.dot_general(vectors, h_slab, (((0,), (1,)), ((), ())), preferred_elem...]
    all_gather x1 -> x0, local copies, waits for them, and re-layouts: 5.34 us -> none  [body(): projected = lax.all_gather(summed, 'col', axis=1, tiled=True)]
    unnamed x2 -> x1, local copies, waits for them, and re-layouts: 0.01 us -> 4.79 us
  transfers between devices with their start and end apart: 1 -> 0, of which waited for: 1 -> 0; matrix products, arithmetic and copies ran while one was open for 0% -> 0% of each run, Pallas kernels for 0% -> 0%
where the time goes in v1:
time: 67.7 us; the launch traced here: 67.6 us
  Pallas kernels  62.8 us (93%)
  local copies, waits for them, and re-layouts  4.79 us (7%)
    pallas_call x1, Pallas kernels, call(): pl.pallas_call(kernel, out_shape=jax.ShapeDtypeStruct((2, 4, 2, 64, NVEC)...  62.8 us
    unnamed x1, local copies, waits for them, and re-layouts  4.79 us

profile of v1, /device:TPU:1, one launch (start us, length us, event | category | flops | bytes accessed | tf_op | source)
XLA Modules:
  0.0 67.6 jit_solution(13135551140925690039)
XLA Ops:
  0.0 62.8 %shard_map.37 = f32[2,4,2,64,1024]{4,3,2,1,0:T(8,128)} custom-call(bf16[6000,512]{1,0:T(8,128)(2,1)} %bitcast.3, bf16[6000,1024]{1,0:T(8,128)(2,1)} %v_hbm.1, bf16[512,1024]{1,0:T(8,128)(2,1)} %l_hbm.1), custom_call_target="tpu_custom_call" | custom-call | flops 6291456000 | bytes 23000000 | tf_op jit(solution)/shard_map/pallas_call | solution.py:264
  62.8 4.8 %copy.5 = f32[1024,1024]{1,0:T(8,128)} copy(f32[1024,1024]{1,0:T(8,128)} %bitcast.2) | data formatting | bytes 8388608

commit v2 on v0

v2 whole, which is shorter than its diff:
```python
import functools

import jax
import jax.numpy as jnp
from jax import lax
from jax.experimental import pallas as pl
from jax.experimental.pallas import tpu as pltpu
from jax.sharding import PartitionSpec as P

MESH = pl.DeviceIdType.MESH
F32 = jnp.float32
BF16 = jnp.bfloat16
DEPTH = 6000
ROWS = 512
HALF = 256
NVEC = 1024
CUTS = ((0, 2048), (2048, 4096), (4096, 6000))
ROTATIONS = ((0, 24), (24, 24), (48, 16))
SWAP, GATHER, PAIR, ROWSUM, PLANE, LINE, OTHER, SENDS = 0, 1, 2, 3, 4, 7, 10, 13
COLS, PAIRED, ROWS_IN, PLANE_IN, LINE_IN, OTHER_IN, ARRIVALS = 4, 5, 6, 9, 21, 33, 35
CONTRACT0 = (((0,), (0,)), ((), ()))


def kernel(h_hbm, v_hbm, l_hbm, out, h, v, ht, gx, l, p, dr, zr, pf, pfr, bhl, rp, rr, lsem, ssem, rsem):
    row, col = lax.axis_index("row"), lax.axis_index("col")
    y, xh = row // 2, row % 2
    z, xl, c = col // 4, (col // 2) % 2, col % 2
    x = xh * 2 + xl

    def dev(dx=0, dy=0, dz=0, core=None, px=None):
        nx = (x + dx) % 4 if px is None else px
        ny, nz = (y + dy) % 4, (z + dz) % 4
        nc = c if core is None else core
        return (ny * 2 + nx // 2, nz * 4 + (nx % 2) * 2 + nc)

    partner = dev(core=1 - c)

    zs = [(z + 2) % 4, (z + 1) % 4, (z + 3) % 4, z]
    lanes = [pl.ds(pl.multiple_of(q * 256, 256), 256) for q in zs]
    loads = []

    def load(src, dst):
        cp = pltpu.make_async_copy(src, dst, lsem.at[len(loads)])
        cp.start()
        loads.append(cp)
        return cp

    first = []
    for lo, hi in CUTS:
        k = pl.ds(lo, hi - lo)
        first.append((load(h_hbm.at[k, :], h.at[k, :]), load(v_hbm.at[k, lanes[0]], v.at[0, k, :])))
    rest = [load(v_hbm.at[:, lanes[s]], v.at[s]) for s in (1, 2, 3)]
    lload = load(l_hbm.at[:, pl.ds(pl.multiple_of(c * 512, 512), 512)], l)

    barrier = pltpu.get_barrier_semaphore()
    peers = [partner]
    for d in (1, 2, 3):
        peers += [dev(dx=d), dev(dy=d), dev(dz=d)]
        for e in (1, 2, 3):
            peers += [dev(dx=d, dy=e), dev(dy=d, dz=e), dev(dz=d, dx=e)]
    for peer in peers:
        pl.semaphore_signal(barrier, inc=1, device_id=peer, device_id_type=MESH)

    def send(src, dst, device, out_sem, in_sem):
        pltpu.make_async_remote_copy(
            src_ref=src, dst_ref=dst, send_sem=ssem.at[out_sem], recv_sem=rsem.at[in_sem], device_id=device, device_id_type=MESH
        ).start()

    def wait(sem, ref):
        pltpu.make_async_copy(ref, ref, sem).wait()

    def multiply(s):
        for j in (0, 1):
            p[s, j] = jnp.dot(ht[pl.ds(j * HALF, HALF), :], v[s], preferred_element_type=F32)

    def swap(s):
        send(p.at[s, 1 - c], dr.at[s], partner, SWAP, s)

    def settle(s):
        wait(rsem.at[s], dr.at[s])
        p[s, c] = p[s, c] + dr[s]

    ours = pl.ds(pl.multiple_of(xl * 128, 128), 128)
    theirs = pl.ds(pl.multiple_of(128 - xl * 128, 128), 128)

    def scatter(s):
        dz = (2, 1, 3, 0)[s]
        send(p.at[s, c, :, theirs], zr.at[2 * s], dev(px=xh * 2 + 1 - xl, dz=dz), GATHER, COLS)
        if dz:
            send(p.at[s, c, :, ours], zr.at[2 * s + 1], dev(dz=dz), GATHER, COLS)

    for i, (lo, hi) in enumerate(CUTS):
        first[i][0].wait()
        first[i][1].wait()
        k = pl.ds(lo, hi - lo)
        ht[:, k] = h[k, :].T
        for j in (0, 1):
            q = jnp.dot(ht[pl.ds(j * HALF, HALF), k], v[0, k, :], preferred_element_type=F32)
            p[0, j] = q if i == 0 else p[0, j] + q
    pl.semaphore_wait(barrier, len(peers))
    swap(0)
    rest[0].wait()
    multiply(1)
    swap(1)
    settle(0)
    scatter(0)
    rest[1].wait()
    multiply(2)
    swap(2)
    settle(1)
    scatter(1)
    rest[2].wait()
    multiply(3)
    swap(3)
    settle(2)
    scatter(2)
    settle(3)
    scatter(3)
    wait(rsem.at[COLS], zr)
    mine = p[3, c, :, ours]
    for i in range(7):
        mine = mine + zr[i]
    pf[...] = mine
    send(pf, pfr, partner, PAIR, PAIRED)

    def split(value, half):
        hi = value.astype(BF16)
        bhl[half, :, pl.ds(0, 128)] = hi
        bhl[half, :, pl.ds(128, 128)] = (value - hi.astype(F32)).astype(BF16)

    split(pf[...], c)
    lload.wait()
    wait(rsem.at[PAIRED], pfr)
    split(pfr[...], 1 - c)
    both = lax.dot_general(l[...], bhl[...].reshape(ROWS, 256), CONTRACT0, preferred_element_type=F32)
    rp[...] = (both[:, :128] + both[:, 128:]).reshape(8, 64, 128)

    R = [pl.ds(a, n) for a, n in ROTATIONS]
    for t in range(3):
        i = 0
        for dx in (0, 2):
            for dy in (0, 1, 3, 2):
                if dx or dy:
                    their_row = ((y + dy) % 4) * 2 + (xh + dx // 2) % 2
                    send(rp.at[their_row, R[t]], rr.at[i, R[t]], dev(dx=dx, dy=dy), ROWSUM, ROWS_IN + t)
                    i += 1

    def lane(qz, qx):
        return pl.ds(pl.multiple_of(qz * 256 + (qx % 2) * 128, 128), 128)

    def wide(qz):
        return pl.ds(pl.multiple_of(qz * 256, 256), 256)

    def set_x(d, g):
        return gx.at[c, (x + d) % 4, (y + g) % 4]

    def set_y(d, g):
        return out.at[c, (y + d) % 4, :, R[1], wide((z + g) % 4)]

    def set_z(d, g):
        qx = (x + g) % 4
        return out.at[c, :, qx // 2, R[2], lane((z + d) % 4, qx)]

    sets = (set_x, set_y, set_z)
    order = (("dz", "dy", "dx"), ("dx", "dz", "dy"), ("dy", "dx", "dz"))
    def spread(half):
        for qx in range(4):
            for qy in range(4):
                for qz in range(4):
                    lanes = pl.ds(qz * 256 + (qx % 2) * 128, 128)
                    out[half, qy, qx // 2, R[0], lanes] = gx[half, qx, qy, qz]

    own = [gx.at[c, x, y, z]] + [out.at[c, y, xh, r, lane(z, x)] for r in R[1:]]

    for t, (_, n) in enumerate(ROTATIONS):
        wait(rsem.at[ROWS_IN + t], rr.at[:, R[t]])
        total = rp[row, R[t]]
        for i in range(7):
            total = total + rr[i, R[t]]
        if t == 0:
            gx[c, x, y, z] = total
        else:
            out[c, y, xh, R[t], lane(z, x)] = total
        for b in (0, 1, 3, 2):
            for a in (1, 3, 2, 0):
                if a or b:
                    device = dev(**{order[t][0]: a, order[t][1]: b})
                    send(own[t], own[t], device, PLANE + t, PLANE_IN + 4 * t + (4 - b) % 4)
    groups = (0, 3, 1, 2)
    for g in groups:
        for t, (_, n) in enumerate(ROTATIONS):
            line = sets[t](0, g)
            wait(rsem.at[PLANE_IN + 4 * t + g], zr.at[pl.ds(0, 4 if g else 3), pl.ds(0, n)])
            for d in (1, 3, 2):
                send(line, line, dev(**{order[t][2]: d}), LINE + t, LINE_IN + 4 * t + g)
            send(line, line, partner, OTHER + t, OTHER_IN + min(t, 1))
    for g in groups:
        for t, (_, n) in enumerate(ROTATIONS):
            wait(rsem.at[LINE_IN + 4 * t + g], zr.at[pl.ds(0, 3), pl.ds(0, 4 * n)])
            for d in (1, 3, 2):
                line = sets[t](d, g)
                send(line, line, partner, OTHER + t, OTHER_IN + min(t, 1))
    low = ROTATIONS[0][1]
    spread(c)
    wait(rsem.at[OTHER_IN], gx.at[1 - c])
    spread(1 - c)
    wait(rsem.at[OTHER_IN + 1], out.at[1 - c, :, :, pl.ds(low, 64 - low), :])
    wait(ssem.at[SWAP], dr)
    wait(ssem.at[GATHER], zr)
    wait(ssem.at[PAIR], pf)
    wait(ssem.at[ROWSUM], rr)
    for t, (_, n) in enumerate(ROTATIONS):
        wait(ssem.at[PLANE + t], zr.at[pl.ds(0, 5), pl.ds(0, 3 * n)])
        wait(ssem.at[LINE + t], zr.at[pl.ds(0, 6), pl.ds(0, 8 * n)])
        wait(ssem.at[OTHER + t], out.at[c, :, :, pl.ds(0, n), :])


def call(h, v, l):
    dma = pltpu.SemaphoreType.DMA
    vmem = pltpu.VMEM
    return pl.pallas_call(
        kernel,
        out_shape=pltpu.VMEM((2, 4, 2, 64, NVEC), F32),
        in_specs=[pl.BlockSpec(memory_space=pltpu.HBM)] * 3,
        out_specs=pl.BlockSpec(memory_space=pltpu.VMEM),
        scratch_shapes=[
            vmem((DEPTH, ROWS), BF16),
            vmem((4, DEPTH, 256), BF16),
            vmem((ROWS, DEPTH), BF16),
            vmem((2, 4, 4, 4, ROTATIONS[0][1], 128), F32),
            vmem((ROWS, 512), BF16),
            vmem((4, 2, HALF, 256), F32),
            vmem((4, HALF, 256), F32),
            vmem((7, HALF, 128), F32),
            vmem((HALF, 128), F32),
            vmem((HALF, 128), F32),
            vmem((2, HALF, 256), BF16),
            vmem((8, 64, 128), F32),
            vmem((7, 64, 128), F32),
            dma((10,)),
            dma((SENDS,)),
            dma((ARRIVALS,)),
        ],
        compiler_params=pltpu.CompilerParams(
            collective_id=0, has_side_effects=True, vmem_limit_bytes=46 * 1024 * 1024
        ),
        cost_estimate=pl.CostEstimate(flops=2 * ROWS * DEPTH * NVEC, bytes_accessed=23000000, transcendentals=0),
    )(h, v, l)


def body(h_slab, vectors, left_rows):
    h, v, l = [pltpu.with_memory_space_constraint(a, pltpu.HBM) for a in (h_slab.T, vectors, left_rows)]
    return call(h, v, l).reshape(NVEC, NVEC)


def solution(mesh):
    in_specs = (P("row", "col"), P("col", None), P("row", None))
    return jax.shard_map(body, mesh=mesh, in_specs=in_specs, out_specs=P(), check_vma=False)
```

time: 135 us -> 51.7 us (0.38)
  blocking collectives: 67.2 us -> 0 us
  Pallas kernels: 0 us -> 49.6 us
  waiting for transfers between devices: 35.4 us -> 0 us
  between operations: 13.4 us -> 0.01 us
  matrix products: 12.1 us -> 0 us
  local copies, waits for them, and re-layouts: 5.58 us -> 2.02 us
    all_to_all x2 -> x0, blocking collectives: 67.2 us -> none  [the longest x1 34 us: sum_at_owner(): lax.all_to_all(cut_along(shard, dim, devices), axis, 0, 0, tiled=True)]
    pallas_call x0 -> x1, Pallas kernels: none -> 49.6 us  [call(): pl.pallas_call(kernel, out_shape=pltpu.VMEM((2, 4, 2, 64, NVEC), F32), in...]
    all_gather x1 -> x0, waiting for transfers between devices: 35.4 us -> none  [body(): projected = lax.all_gather(summed, 'col', axis=1, tiled=True)]
    dot_general x2 -> x0, matrix products: 12.1 us -> none  [the longest x1 11.5 us: body(): lax.dot_general(vectors, h_slab, (((0,), (1,)), ((), ())), preferred_elem...]
    all_gather x1 -> x0, local copies, waits for them, and re-layouts: 5.34 us -> none  [body(): projected = lax.all_gather(summed, 'col', axis=1, tiled=True)]
    unnamed x2 -> x1, local copies, waits for them, and re-layouts: 0.01 us -> 2.02 us
  transfers between devices with their start and end apart: 1 -> 0, of which waited for: 1 -> 0; matrix products, arithmetic and copies ran while one was open for 0% -> 0% of each run, Pallas kernels for 0% -> 0%
where the time goes in v2:
time: 51.7 us; the launch traced here: 51.6 us
  Pallas kernels  49.6 us (96%)
  local copies, waits for them, and re-layouts  2.02 us (4%)
    pallas_call x1, Pallas kernels, call(): pl.pallas_call(kernel, out_shape=pltpu.VMEM((2, 4, 2, 64, NVEC), F32), in...  49.6 us
    unnamed x1, local copies, waits for them, and re-layouts  2.02 us

profile of v2, /device:TPU:1, one launch (start us, length us, event | category | flops | bytes accessed | tf_op | source)
XLA Modules:
  0.0 51.6 jit_solution(8914310914424290863)
XLA Ops:
  0.0 49.6 %shard_map.37 = f32[2,4,2,64,1024]{4,3,2,1,0:T(8,128)S(1)} custom-call(bf16[6000,512]{1,0:T(8,128)(2,1)} %bitcast.3, bf16[6000,1024]{1,0:T(8,128)(2,1)} %v_hbm.1, bf16[512,1024]{1,0:T(8,128)(2,1)} %l_hbm.1), custom_call_target="tpu_custom_call" | custom-call | flops 6291456000 | bytes 23000000 | tf_op jit(solution)/shard_map/pallas_call | solution.py:221
  49.6 2.0 %copy.5 = f32[1024,1024]{1,0:T(8,128)} copy(f32[1024,1024]{1,0:T(8,128)S(1)} %bitcast.2) | data formatting | bytes 8388608

commit v3 on v2

--- a/solution.py
+++ b/solution.py
@@ -17,11 +17,13 @@
 CUTS = ((0, 2048), (2048, 4096), (4096, 6000))
 ROTATIONS = ((0, 24), (24, 24), (48, 16))
 SWAP, GATHER, PAIR, ROWSUM, PLANE, LINE, OTHER, SENDS = 0, 1, 2, 3, 4, 7, 10, 13
-COLS, PAIRED, ROWS_IN, PLANE_IN, LINE_IN, OTHER_IN, ARRIVALS = 4, 5, 6, 9, 21, 33, 35
+COLS, PAIRED, ROWS_IN, PLANE_IN, LINE_IN, OTHER_IN, PASSED, ARRIVALS = 8, 9, 10, 13, 25, 37, 39, 41
+UNITS = ((0, 0), (0, 1), (1, 0), (2, 0), (1, 1), (2, 1), (3, 0), (3, 1))
+SETTLE = ((), (0,), (1,), (), (2,), (3,), (4,), (5, 6, 7))
 CONTRACT0 = (((0,), (0,)), ((), ()))
 
 
-def kernel(h_hbm, v_hbm, l_hbm, out, h, v, ht, gx, l, p, dr, zr, pf, pfr, bhl, rp, rr, lsem, ssem, rsem):
+def kernel(h_hbm, v_hbm, l_hbm, out, h, v, gx, l, p, dr, zr, zf, pf, pfr, bhl, rp, rr, lsem, ssem, rsem):
     row, col = lax.axis_index("row"), lax.axis_index("col")
     y, xh = row // 2, row % 2
     z, xl, c = col // 4, (col // 2) % 2, col % 2
@@ -45,10 +47,20 @@
         loads.append(cp)
         return cp
 
+    ours = pl.ds(pl.multiple_of(xl * 128, 128), 128)
+    theirs = pl.ds(pl.multiple_of(128 - xl * 128, 128), 128)
+    mine_k = pl.ds(pl.multiple_of(c * HALF, HALF), HALF)
+    other_k = pl.ds(pl.multiple_of(HALF - c * HALF, HALF), HALF)
+
+    def columns(s, which):
+        start = zs[s] * 256 + (xl if which else 1 - xl) * 128
+        return pl.ds(pl.multiple_of(start, 128), 128)
+
     first = []
     for lo, hi in CUTS:
         k = pl.ds(lo, hi - lo)
-        first.append((load(h_hbm.at[k, :], h.at[k, :]), load(v_hbm.at[k, lanes[0]], v.at[0, k, :])))
+        first.append((load(h_hbm.at[k, :], h.at[k, :]), load(v_hbm.at[k, columns(0, 0)], v.at[0, k, theirs])))
+    later = load(v_hbm.at[:, columns(0, 1)], v.at[0, :, ours])
     rest = [load(v_hbm.at[:, lanes[s]], v.at[s]) for s in (1, 2, 3)]
     lload = load(l_hbm.at[:, pl.ds(pl.multiple_of(c * 512, 512), 512)], l)
 
@@ -69,70 +81,78 @@
     def wait(sem, ref):
         pltpu.make_async_copy(ref, ref, sem).wait()
 
-    def multiply(s):
-        for j in (0, 1):
-            p[s, j] = jnp.dot(ht[pl.ds(j * HALF, HALF), :], v[s], preferred_element_type=F32)
-
-    def swap(s):
-        send(p.at[s, 1 - c], dr.at[s], partner, SWAP, s)
-
-    def settle(s):
-        wait(rsem.at[s], dr.at[s])
-        p[s, c] = p[s, c] + dr[s]
-
-    ours = pl.ds(pl.multiple_of(xl * 128, 128), 128)
-    theirs = pl.ds(pl.multiple_of(128 - xl * 128, 128), 128)
-
-    def scatter(s):
-        dz = (2, 1, 3, 0)[s]
-        send(p.at[s, c, :, theirs], zr.at[2 * s], dev(px=xh * 2 + 1 - xl, dz=dz), GATHER, COLS)
-        if dz:
-            send(p.at[s, c, :, ours], zr.at[2 * s + 1], dev(dz=dz), GATHER, COLS)
-
-    for i, (lo, hi) in enumerate(CUTS):
-        first[i][0].wait()
-        first[i][1].wait()
-        k = pl.ds(lo, hi - lo)
-        ht[:, k] = h[k, :].T
-        for j in (0, 1):
-            q = jnp.dot(ht[pl.ds(j * HALF, HALF), k], v[0, k, :], preferred_element_type=F32)
-            p[0, j] = q if i == 0 else p[0, j] + q
-    pl.semaphore_wait(barrier, len(peers))
-    swap(0)
-    rest[0].wait()
-    multiply(1)
-    swap(1)
-    settle(0)
-    scatter(0)
-    rest[1].wait()
-    multiply(2)
-    swap(2)
-    settle(1)
-    scatter(1)
-    rest[2].wait()
-    multiply(3)
-    swap(3)
-    settle(2)
-    scatter(2)
-    settle(3)
-    scatter(3)
+    def multiply(u, s, which):
+        mine = ours if which else theirs
+        if u:
+            p[u] = lax.dot_general(v[s, :, mine], h[...], CONTRACT0, preferred_element_type=F32)
+            return
+        for i, (lo, hi) in enumerate(CUTS):
+            for cp in first[i]:
+                cp.wait()
+            k = pl.ds(lo, hi - lo)
+            q = lax.dot_general(v[s, k, mine], h[k, :], CONTRACT0, preferred_element_type=F32)
+            p[u] = p[u] + q if i else q
+
+    def settle(u):
+        wait(rsem.at[u], dr.at[u])
+        p[u, :, mine_k] = p[u, :, mine_k] + dr[u]
+
+    up, down = dev(dz=1), dev(dz=3)
+    low, high = pl.ds(0, 64), pl.ds(64, 64)
+
+    def owner(u):
+        s, which = UNITS[u]
+        return dev(px=x if which else xh * 2 + 1 - xl, dz=(2, 1, 3, 0)[s])
+
+    def scatter(u, rows=None):
+        s, which = UNITS[u]
+        if s == 0:
+            send(p.at[u, low, mine_k], zf.at[0, which], up, GATHER, PASSED)
+            send(p.at[u, high, mine_k], zf.at[1, which], down, GATHER, PASSED + 1)
+        elif s == 3:
+            if which == 0:
+                send(p.at[u, :, mine_k], zr.at[4], owner(u), GATHER, COLS)
+        else:
+            rows = rows or (None, high, low)[s]
+            send(p.at[u, rows, mine_k], zr.at[2 * s - 2 + which, rows], owner(u), GATHER, COLS)
+
+    loaded = set()
+    for u, (s, which) in enumerate(UNITS):
+        if u == 1:
+            later.wait()
+        if s and s not in loaded:
+            rest[s - 1].wait()
+            loaded.add(s)
+        multiply(u, s, which)
+        if u == 0:
+            pl.semaphore_wait(barrier, len(peers))
+        send(p.at[u, :, other_k], dr.at[u], partner, SWAP, u)
+        for w in SETTLE[u]:
+            settle(w)
+            scatter(w)
+    for i, rows in enumerate((low, high)):
+        wait(rsem.at[PASSED + i], zf.at[i])
+        for u, (s, which) in enumerate(UNITS):
+            if s == i + 1:
+                p[u, rows, mine_k] = p[u, rows, mine_k] + zf[i, which]
+                scatter(u, rows)
     wait(rsem.at[COLS], zr)
-    mine = p[3, c, :, ours]
-    for i in range(7):
+    mine = p[7, :, mine_k]
+    for i in range(5):
         mine = mine + zr[i]
     pf[...] = mine
     send(pf, pfr, partner, PAIR, PAIRED)
 
-    def split(value, half):
+    def split(value, k):
         hi = value.astype(BF16)
-        bhl[half, :, pl.ds(0, 128)] = hi
-        bhl[half, :, pl.ds(128, 128)] = (value - hi.astype(F32)).astype(BF16)
-
-    split(pf[...], c)
+        bhl[pl.ds(0, 128), k] = hi
+        bhl[pl.ds(128, 128), k] = (value - hi.astype(F32)).astype(BF16)
+
+    split(pf[...], mine_k)
     lload.wait()
     wait(rsem.at[PAIRED], pfr)
-    split(pfr[...], 1 - c)
-    both = lax.dot_general(l[...], bhl[...].reshape(ROWS, 256), CONTRACT0, preferred_element_type=F32)
+    split(pfr[...], other_k)
+    both = lax.dot_general(l[...], bhl[...], (((0,), (1,)), ((), ())), preferred_element_type=F32)
     rp[...] = (both[:, :128] + both[:, 128:]).reshape(8, 64, 128)
 
     R = [pl.ds(a, n) for a, n in ROTATIONS]
@@ -190,13 +210,13 @@
     for g in groups:
         for t, (_, n) in enumerate(ROTATIONS):
             line = sets[t](0, g)
-            wait(rsem.at[PLANE_IN + 4 * t + g], zr.at[pl.ds(0, 4 if g else 3), pl.ds(0, n)])
+            wait(rsem.at[PLANE_IN + 4 * t + g], dr.at[pl.ds(0, 4 if g else 3), pl.ds(0, n), pl.ds(0, 128)])
             for d in (1, 3, 2):
                 send(line, line, dev(**{order[t][2]: d}), LINE + t, LINE_IN + 4 * t + g)
             send(line, line, partner, OTHER + t, OTHER_IN + min(t, 1))
     for g in groups:
         for t, (_, n) in enumerate(ROTATIONS):
-            wait(rsem.at[LINE_IN + 4 * t + g], zr.at[pl.ds(0, 3), pl.ds(0, 4 * n)])
+            wait(rsem.at[LINE_IN + 4 * t + g], dr.at[pl.ds(0, 3), pl.ds(0, 2 * n)])
             for d in (1, 3, 2):
                 line = sets[t](d, g)
                 send(line, line, partner, OTHER + t, OTHER_IN + min(t, 1))
@@ -206,12 +226,12 @@
     spread(1 - c)
     wait(rsem.at[OTHER_IN + 1], out.at[1 - c, :, :, pl.ds(low, 64 - low), :])
     wait(ssem.at[SWAP], dr)
-    wait(ssem.at[GATHER], zr)
+    wait(ssem.at[GATHER], dr.at[pl.ds(0, 7)])
     wait(ssem.at[PAIR], pf)
     wait(ssem.at[ROWSUM], rr)
     for t, (_, n) in enumerate(ROTATIONS):
-        wait(ssem.at[PLANE + t], zr.at[pl.ds(0, 5), pl.ds(0, 3 * n)])
-        wait(ssem.at[LINE + t], zr.at[pl.ds(0, 6), pl.ds(0, 8 * n)])
+        wait(ssem.at[PLANE + t], dr.at[pl.ds(0, 5), pl.ds(0, 3 * n), pl.ds(0, 128)])
+        wait(ssem.at[LINE + t], dr.at[pl.ds(0, 6), pl.ds(0, 4 * n)])
         wait(ssem.at[OTHER + t], out.at[c, :, :, pl.ds(0, n), :])
 
 
@@ -226,18 +246,18 @@
         scratch_shapes=[
             vmem((DEPTH, ROWS), BF16),
             vmem((4, DEPTH, 256), BF16),
-            vmem((ROWS, DEPTH), BF16),
             vmem((2, 4, 4, 4, ROTATIONS[0][1], 128), F32),
             vmem((ROWS, 512), BF16),
-            vmem((4, 2, HALF, 256), F32),
-            vmem((4, HALF, 256), F32),
-            vmem((7, HALF, 128), F32),
-            vmem((HALF, 128), F32),
-            vmem((HALF, 128), F32),
-            vmem((2, HALF, 256), BF16),
+            vmem((8, 128, ROWS), F32),
+            vmem((8, 128, HALF), F32),
+            vmem((5, 128, HALF), F32),
+            vmem((2, 2, 64, HALF), F32),
+            vmem((128, HALF), F32),
+            vmem((128, HALF), F32),
+            vmem((2 * 128, ROWS), BF16),
             vmem((8, 64, 128), F32),
             vmem((7, 64, 128), F32),
-            dma((10,)),
+            dma((11,)),
             dma((SENDS,)),
             dma((ARRIVALS,)),
         ],

time: 51.7 us -> 51.4 us (level)
  no operation moved by 1% of the time
where the time goes in v3:
time: 51.4 us; the launch traced here: 51.3 us
  Pallas kernels  49.3 us (96%)
  local copies, waits for them, and re-layouts  2.02 us (4%)
    pallas_call x1, Pallas kernels, call(): pl.pallas_call(kernel, out_shape=pltpu.VMEM((2, 4, 2, 64, NVEC), F32), in...  49.3 us
    unnamed x1, local copies, waits for them, and re-layouts  2.02 us

profile of v3, /device:TPU:1, one launch (start us, length us, event | category | flops | bytes accessed | tf_op | source)
XLA Modules:
  0.0 51.3 jit_solution(1275387831913780540)
XLA Ops:
  0.0 49.3 %shard_map.37 = f32[2,4,2,64,1024]{4,3,2,1,0:T(8,128)S(1)} custom-call(bf16[6000,512]{1,0:T(8,128)(2,1)} %bitcast.3, bf16[6000,1024]{1,0:T(8,128)(2,1)} %v_hbm.1, bf16[512,1024]{1,0:T(8,128)(2,1)} %l_hbm.1), custom_call_target="tpu_custom_call" | custom-call | flops 6291456000 | bytes 23000000 | tf_op jit(solution)/shard_map/pallas_call | solution.py:241
  49.3 2.0 %copy.5 = f32[1024,1024]{1,0:T(8,128)} copy(f32[1024,1024]{1,0:T(8,128)S(1)} %bitcast.2) | data formatting | bytes 8388608

commit v4 on v3

--- a/solution.py
+++ b/solution.py
@@ -18,8 +18,8 @@
 ROTATIONS = ((0, 24), (24, 24), (48, 16))
 SWAP, GATHER, PAIR, ROWSUM, PLANE, LINE, OTHER, SENDS = 0, 1, 2, 3, 4, 7, 10, 13
 COLS, PAIRED, ROWS_IN, PLANE_IN, LINE_IN, OTHER_IN, PASSED, ARRIVALS = 8, 9, 10, 13, 25, 37, 39, 41
-UNITS = ((0, 0), (0, 1), (1, 0), (2, 0), (1, 1), (2, 1), (3, 0), (3, 1))
-SETTLE = ((), (0,), (1,), (), (2,), (3,), (4,), (5, 6, 7))
+UNITS = ((3, 0), (0, 0), (0, 1), (1, 0), (2, 0), (1, 1), (2, 1), (3, 1))
+SETTLE = ((), (0,), (1,), (2,), (3,), (4,), (5,), (6,))
 CONTRACT0 = (((0,), (0,)), ((), ()))
 
 
@@ -59,9 +59,9 @@
     first = []
     for lo, hi in CUTS:
         k = pl.ds(lo, hi - lo)
-        first.append((load(h_hbm.at[k, :], h.at[k, :]), load(v_hbm.at[k, columns(0, 0)], v.at[0, k, theirs])))
-    later = load(v_hbm.at[:, columns(0, 1)], v.at[0, :, ours])
-    rest = [load(v_hbm.at[:, lanes[s]], v.at[s]) for s in (1, 2, 3)]
+        first.append((load(h_hbm.at[k, :], h.at[k, :]), load(v_hbm.at[k, columns(3, 0)], v.at[3, k, theirs])))
+    rest = [load(v_hbm.at[:, lanes[s]], v.at[s]) for s in (0, 1, 2)]
+    rest.append(load(v_hbm.at[:, columns(3, 1)], v.at[3, :, ours]))
     lload = load(l_hbm.at[:, pl.ds(pl.multiple_of(c * 512, 512), 512)], l)
 
     barrier = pltpu.get_barrier_semaphore()
@@ -118,10 +118,8 @@
 
     loaded = set()
     for u, (s, which) in enumerate(UNITS):
-        if u == 1:
-            later.wait()
-        if s and s not in loaded:
-            rest[s - 1].wait()
+        if u and s not in loaded:
+            rest[s].wait()
             loaded.add(s)
         multiply(u, s, which)
         if u == 0:
@@ -136,6 +134,7 @@
             if s == i + 1:
                 p[u, rows, mine_k] = p[u, rows, mine_k] + zf[i, which]
                 scatter(u, rows)
+    settle(7)
     wait(rsem.at[COLS], zr)
     mine = p[7, :, mine_k]
     for i in range(5):

time: 51.4 us -> 50.3 us (0.979)
  Pallas kernels: 49.3 us -> 48.2 us
    pallas_call x1, Pallas kernels: 49.3 us -> 48.2 us  [call(): pl.pallas_call(kernel, out_shape=pltpu.VMEM((2, 4, 2, 64, NVEC), F32), in...]
where the time goes in v4:
time: 50.3 us; the launch traced here: 50.2 us
  Pallas kernels  48.2 us (96%)
  local copies, waits for them, and re-layouts  2.02 us (4%)
    pallas_call x1, Pallas kernels, call(): pl.pallas_call(kernel, out_shape=pltpu.VMEM((2, 4, 2, 64, NVEC), F32), in...  48.2 us
    unnamed x1, local copies, waits for them, and re-layouts  2.02 us

profile of v4, /device:TPU:1, one launch (start us, length us, event | category | flops | bytes accessed | tf_op | source)
XLA Modules:
  0.0 50.2 jit_solution(14988002574854889839)
XLA Ops:
  0.0 48.2 %shard_map.37 = f32[2,4,2,64,1024]{4,3,2,1,0:T(8,128)S(1)} custom-call(bf16[6000,512]{1,0:T(8,128)(2,1)} %bitcast.3, bf16[6000,1024]{1,0:T(8,128)(2,1)} %v_hbm.1, bf16[512,1024]{1,0:T(8,128)(2,1)} %l_hbm.1), custom_call_target="tpu_custom_call" | custom-call | flops 6291456000 | bytes 23000000 | tf_op jit(solution)/shard_map/pallas_call | solution.py:240
  48.2 2.0 %copy.5 = f32[1024,1024]{1,0:T(8,128)} copy(f32[1024,1024]{1,0:T(8,128)S(1)} %bitcast.2) | data formatting | bytes 8388608

commit v5 on v4

--- a/solution.py
+++ b/solution.py
@@ -157,8 +157,8 @@
     R = [pl.ds(a, n) for a, n in ROTATIONS]
     for t in range(3):
         i = 0
-        for dx in (0, 2):
-            for dy in (0, 1, 3, 2):
+        for dx in (2, 0):
+            for dy in (2, 1, 3, 0):
                 if dx or dy:
                     their_row = ((y + dy) % 4) * 2 + (xh + dx // 2) % 2
                     send(rp.at[their_row, R[t]], rr.at[i, R[t]], dev(dx=dx, dy=dy), ROWSUM, ROWS_IN + t)

time: 50.3 us -> 49.5 us (0.984)
  Pallas kernels: 48.2 us -> 47.3 us
    pallas_call x1, Pallas kernels: 48.2 us -> 47.3 us  [call(): pl.pallas_call(kernel, out_shape=pltpu.VMEM((2, 4, 2, 64, NVEC), F32), in...]
where the time goes in v5:
time: 49.5 us; the launch traced here: 49.4 us
  Pallas kernels  47.3 us (96%)
  local copies, waits for them, and re-layouts  2.02 us (4%)
    pallas_call x1, Pallas kernels, call(): pl.pallas_call(kernel, out_shape=pltpu.VMEM((2, 4, 2, 64, NVEC), F32), in...  47.3 us
    unnamed x1, local copies, waits for them, and re-layouts  2.02 us

profile of v5, /device:TPU:1, one launch (start us, length us, event | category | flops | bytes accessed | tf_op | source)
XLA Modules:
  0.0 49.4 jit_solution(7686905874430666677)
XLA Ops:
  0.0 47.3 %shard_map.37 = f32[2,4,2,64,1024]{4,3,2,1,0:T(8,128)S(1)} custom-call(bf16[6000,512]{1,0:T(8,128)(2,1)} %bitcast.3, bf16[6000,1024]{1,0:T(8,128)(2,1)} %v_hbm.1, bf16[512,1024]{1,0:T(8,128)(2,1)} %l_hbm.1), custom_call_target="tpu_custom_call" | custom-call | flops 6291456000 | bytes 23000000 | tf_op jit(solution)/shard_map/pallas_call | solution.py:240
  47.4 2.0 %copy.5 = f32[1024,1024]{1,0:T(8,128)} copy(f32[1024,1024]{1,0:T(8,128)S(1)} %bitcast.2) | data formatting | bytes 8388608
